TPU v7x, 32 devices: a whole 2x2x4 slice. The times are simulated.
32 devices in a mesh: north: 4 (over x, core), east: 8 (over z, y).
Axes of the slice: x: 2, y: 2, z: 4, core: 2. Of those that a mesh axis runs over, the one named last changes fastest.
Arguments:
- left_factor: bfloat16 [4096, 2048], P('north', 'east'), may hold values from -6 to 6
- right_factor: bfloat16 [2048, 4096], P('north', 'east'), may hold values from -0.125 to 0.125
Outputs:
- updated: float32 [4096, 4096], P('north', 'east')
All inputs are finite; a program needn't handle non-finite values.
Results may differ from a plain program's by a relative error of at most 0.0003.
Values may be sent and summed in bfloat16 or wider, within the bound.
A program may use at most 128 MiB of HBM per device.

v0:
```python
import jax
import jax.numpy as jnp
from jax import lax
from jax.sharding import PartitionSpec as P


def over_all(piece, axis, dim, lap, start):
    def gathered(part):
        return lax.all_gather(part, axis, axis=dim, tiled=True)

    return lap(start, jax.tree.map(gathered, piece), jnp.int32(0))


def absorb_panel(carry, left_panel, right_panel):
    return carry + jnp.dot(left_panel, right_panel, preferred_element_type=jnp.float32)


def shards(left_factor, right_factor):
    begin = jnp.zeros((left_factor.shape[0], right_factor.shape[1]), jnp.float32)
    left_line = lax.all_gather(left_factor, "east", axis=1, tiled=True)

    def take_rows(carry, piece, start):
        left_piece = lax.dynamic_slice_in_dim(left_line, start, piece.shape[0], axis=1)
        return absorb_panel(carry, left_piece, piece)

    total = over_all(right_factor, "north", 0, take_rows, begin)
    updated = total
    row_power = lax.psum(jnp.sum(updated * updated, axis=1), "east")
    updated = (
        updated * lax.rsqrt(row_power / (updated.shape[1] * lax.axis_size("east")) + 1e-06)[:, None]
    )
    return updated


def solution(mesh):
    placed = (P("north", "east"), P("north", "east"))
    return jax.shard_map(
        shards, mesh=mesh, in_specs=placed, out_specs=P("north", "east"), check_vma=False
    )
```

profile of v0, /device:TPU:0, one launch (start us, length us, event | category | flops | bytes accessed | tf_op | source)
XLA Modules:
  0.0 146.8 jit_solution(11622587532451686640)
XLA Ops:
  6.5 0.0 all-gather.5.cloned.1.call-start
  6.5 0.7 all-gather.5.cloned.1.call-update
  7.3 0.0 all-gather.3.cloned.1.call-start
  7.3 0.7 all-gather.3.cloned.1.call-update
  8.0 26.1 %all-gather.5.cloned.1.call-done = bf16[2048,512]{1,0:T(8,128)(2,1)} async-done(((bf16[512,512]{1,0:T(8,128)(2,1)}), bf16[2048,512]{1,0:T(8,128)(2,1)}) %all-gather.5.cloned.1.call-update) | async-done | bytes 2097168 | tf_op jit(solution)/shard_map/all_gather | solution.py:9
  34.1 76.8 %all-gather.3.cloned.1.call-done = bf16[1024,2048]{1,0:T(8,128)(2,1)} async-done(((bf16[1024,256]{1,0:T(8,128)(2,1)}), bf16[1024,2048]{1,0:T(8,128)(2,1)}) %all-gather.3.cloned.1.call-update) | async-done | bytes 4194320 | tf_op jit(solution)/shard_map/all_gather | solution.py:20
  110.9 6.6 %multiply_reduce_fusion = (f32[1024]{0:T(1024)S(1)}, f32[1024,512]{0,1:T(8,128)}) fusion(bf16[1024,2048]{1,0:T(8,128)(2,1)} %all-gather.3.cloned.1.call-done, bf16[2048,512]{1,0:T(8,128)(2,1)} %all-gather.5.cloned.1.call-done), kind=kOutput, calls=%fused_computation | convolution fusion | flops 2148531200 | bytes 8392704 | tf_op jit(solution)/shard_map/dot_general | solution.py:15
  117.5 18.8 %psum.7 = f32[1024]{0:T(1024)S(1)} all-reduce(f32[1024]{0:T(1024)S(1)} %get-tuple-element.5), channel_id=1, replica_groups=mesh['north'=4,'east'=8] {'east'}, use_global_device_ids=true, to_apply=%region_1.0 | all-reduce | flops 1024 | bytes 8192 | tf_op jit(solution)/shard_map/psum | solution.py:28
  136.3 1.8 %broadcast_multiply_fusion = f32[1024,512]{0,1:T(8,128)S(1)} fusion(f32[1024,512]{0,1:T(8,128)} %get-tuple-element.6, f32[1024]{0:T(1024)S(1)} %add_rsqrt_fusion), kind=kLoop, calls=%fused_computation.1 | loop fusion | flops 524288 | bytes 4198400 | tf_op jit(solution)/shard_map/mul | solution.py:30
  138.1 1.8 %copy.3 = f32[1024,512]{1,0:T(8,128)} copy(f32[1024,512]{0,1:T(8,128)S(1)} %broadcast_multiply_fusion) | data formatting | bytes 4194304 | tf_op jit(solution)/shard_map/mul | solution.py:30
  (1 shorter events, 0.0 us)
Async XLA Ops:
  6.5 27.6 %all-gather.5.cloned.1.call-start = ((), (), s32[]{:S(2)}) async-start(), calls=%async_computation.1 | async-start | bytes 2621440 | tf_op jit(solution)/shard_map/all_gather | solution.py:9
  7.3 103.7 %all-gather.3.cloned.1.call-start = ((), (), s32[]{:S(2)}) async-start(), calls=%async_computation | async-start | bytes 4718592 | tf_op jit(solution)/shard_map/all_gather | solution.py:20
Sparse Core Ops, SparseCore 0:
  8.9 25.1 all-gather.4
  36.2 74.7 all-gather.2
where the time goes:
time: 147 us
  waiting for transfers between devices  104 us (71%)
  blocking collectives  18.8 us (13%)
  between operations  13.4 us (9%)
  matrix products  6.55 us (4%)
  other arithmetic  1.82 us (1%)
  local copies, waits for them, and re-layouts  1.81 us (1%)
    all_gather x1, waiting for transfers between devices, shards(): left_line = lax.all_gather(left_factor, 'east', axis=1, tiled=True)  76.8 us
    all_gather x1, waiting for transfers between devices, gathered(): return lax.all_gather(part, axis, axis=dim, tiled=True)  26.1 us
    psum x1, blocking collectives, shards(): row_power = lax.psum(jnp.sum(updated * updated, axis=1), 'east')  18.8 us
    dot_general x1, matrix products, absorb_panel(): jnp.dot(left_panel, right_panel, preferred_element_type=jnp.float32)  6.55 us
  transfers between devices with their start and end apart: 2, of which 2 were waited for; matrix products, arithmetic and copies ran while one was open for 0% of the time, Pallas kernels for 0%

commit v1 on v0

v1 whole, which is shorter than its diff:
```python
import functools

import jax
import jax.numpy as jnp
from jax import lax
from jax.experimental import pallas as pl
from jax.experimental.pallas import tpu as pltpu
from jax.sharding import PartitionSpec as P

MESH = pl.DeviceIdType.MESH
PIECES = 2
LANES = 128


def ring_order(ys, zs):
    if ys < 2 or zs % 2:
        return list(range(ys * zs))
    walk = [(z, 0) for z in range(zs)]
    for turn, z in enumerate(reversed(range(zs))):
        line = range(1, ys) if turn % 2 == 0 else reversed(range(1, ys))
        walk += [(z, y) for y in line]
    return [z * ys + y for z, y in walk]


def look_up(table, index):
    found = jnp.int32(table[0])
    for i in range(1, len(table)):
        found = jnp.where(index == i, jnp.int32(table[i]), found)
    return found


def kernel(
    xs, order, a_hbm, b_hbm, out, own, ring, right, sums_own, sums_in,
    load, a_send, a_recv, x_send, x_recv, c_send, c_recv, s_send, s_recv,
):
    n = len(order)
    rows, depth = own.shape
    half = rows // 2
    piece = half // PIECES
    b_rows = b_hbm.shape[0]
    columns = out.shape[1]

    me_north, me = lax.axis_index("north"), lax.axis_index("east")
    x, core = lax.div(me_north, 2), lax.rem(me_north, 2)
    place = [0] * n
    for p, e in enumerate(order):
        place[e] = p
    spot = look_up(place, me)

    def at(steps):
        return look_up(order, lax.rem(spot + (steps + n), n))

    toward = (at(1), at(-1))
    partner = 2 * x + 1 - core

    def x_at(steps):
        return 2 * lax.rem(x + (steps + xs), xs) + core

    load_a = pltpu.make_async_copy(a_hbm, own, load.at[0])
    load_a.start()
    b_own = right.at[pl.ds(pl.multiple_of(me_north * b_rows, b_rows), b_rows)]
    load_b = pltpu.make_async_copy(b_hbm, b_own, load.at[1])
    load_b.start()

    greeted = [(me_north, e) for e in (toward if n > 2 else toward[:1])]
    greeted.append((partner, me))
    if xs > 1:
        greeted.append((x_at(1), me))
    if xs > 2:
        greeted.append((x_at(-1), me))
    barrier = pltpu.get_barrier_semaphore()
    for device in greeted:
        pl.semaphore_signal(barrier, inc=1, device_id=device, device_id_type=MESH)
    pl.semaphore_wait(barrier, len(greeted))

    def a_copy(step, d, c):
        if step == 0:
            source = own.at[pl.ds(d * half + c * piece, piece)]
        else:
            source = ring.at[d, step - 1, pl.ds(c * piece, piece)]
        return pltpu.make_async_remote_copy(
            src_ref=source,
            dst_ref=ring.at[d, step, pl.ds(c * piece, piece)],
            send_sem=a_send.at[d, step, c],
            recv_sem=a_recv.at[d, step, c],
            device_id=(me_north, toward[d]),
            device_id_type=MESH,
        )

    def b_copy(t, target, send, recv, source_core):
        owner = 2 * lax.rem(x - t + xs, xs) + source_core
        block = right.at[pl.ds(pl.multiple_of(owner * b_rows, b_rows), b_rows)]
        return pltpu.make_async_remote_copy(
            src_ref=block, dst_ref=block, send_sem=send.at[t], recv_sem=recv.at[t],
            device_id=(target, me), device_id_type=MESH,
        )

    a_copies = {(s, d, c): a_copy(s, d, c) for s in range(n - 1) for d in range(2) for c in range(PIECES)}
    x_copies = [b_copy(t, x_at(1), x_send, x_recv, core) for t in range(xs - 1)]
    c_copies = [b_copy(t, partner, c_send, c_recv, core) for t in range(xs)]

    load_a.wait()
    for c in range(PIECES):
        for d in range(2):
            a_copies[0, d, c].start()
    load_b.wait()
    if xs > 1:
        x_copies[0].start()
    c_copies[0].start()

    def multiply(j, d, first, start, count):
        owner = at(-j if d == 0 else j)
        b = right.at[pl.ds(pl.multiple_of(owner * depth, depth), depth)]

        @pl.loop(0, count // piece)
        def _(r):
            begin = pl.multiple_of(start + r * piece, piece)
            a_rows = pl.ds(begin, piece)
            o_rows = pl.ds(pl.multiple_of(d * half + begin, piece), piece)
            a = own[o_rows, :] if j == 0 else ring[d, j - 1, a_rows, :]
            term = jnp.dot(a, b[...], preferred_element_type=jnp.float32)
            if first:
                out[o_rows, :] = term
            else:
                out[o_rows, :] += term

    state = {"b": 1, "done": 0}

    def b_stage():
        t = state["b"]
        x_copies[t - 1].wait_recv()
        if t < xs - 1:
            x_copies[t].start()
        c_copies[t].start()
        state["b"] += 1

    def compute(limit, most):
        for _ in range(most):
            j = state["done"]
            if j > limit:
                return
            if j == 0:
                for t in range(xs):
                    c_copies[t].wait_recv()
            for d in range(2):
                multiply(j, d, j == 0, 0, half)
            state["done"] += 1

    for s in range(n - 2):
        for c in range(PIECES):
            for d in range(2):
                a_copies[s, d, c].wait_recv()
                a_copies[s + 1, d, c].start()
        if s % 2 == 1 and state["b"] < xs:
            b_stage()
        elif state["b"] >= xs:
            compute(s + 1, 2)
    while state["b"] < xs:
        b_stage()
    compute(n - 2, n)

    for c in range(PIECES):
        for d in range(2):
            a_copies[n - 2, d, c].wait_recv()
            multiply(n - 1, d, False, c * piece, piece)
            begin = d * half + c * piece
            block = out[pl.ds(begin, piece), :]
            block = block * block
            narrow = block[:, :LANES]
            for k in range(LANES, columns, LANES):
                narrow = narrow + block[:, k:k + LANES]
            sums_own[:, pl.ds(begin, piece)] = jnp.sum(narrow.T, axis=0, keepdims=True)

    for copy in a_copies.values():
        copy.wait_send()
    for copy in x_copies + c_copies:
        copy.wait_send()

    s_copies = [
        pltpu.make_async_remote_copy(
            src_ref=sums_own, dst_ref=sums_in.at[k - 1],
            send_sem=s_send.at[k - 1], recv_sem=s_recv.at[k - 1],
            device_id=(me_north, lax.rem(me + k, n)), device_id_type=MESH,
        )
        for k in range(1, n)
    ]
    for copy in s_copies:
        copy.start()
    for copy in s_copies:
        copy.wait_recv()
    power = sums_own[...]
    for k in range(n - 1):
        power = power + sums_in[k]
    scale = lax.rsqrt(power / (columns * n) + 1e-06)
    for begin in range(0, rows, piece):
        gain = jnp.broadcast_to(scale[:, begin:begin + piece], (LANES, piece)).T
        for k in range(0, columns, LANES):
            out[pl.ds(begin, piece), k:k + LANES] *= gain
    for copy in s_copies:
        copy.wait_send()


def shards(xs, order, left, right):
    n = len(order)
    rows, depth = left.shape
    b_rows, columns = right.shape
    half = rows // 2
    steps = n - 1
    total = 2 * (rows * depth * n + b_rows * columns * 2 * xs) + 4 * rows * columns
    dma = pltpu.SemaphoreType.DMA
    return pl.pallas_call(
        functools.partial(kernel, xs, order),
        out_shape=jax.ShapeDtypeStruct((rows, columns), jnp.float32),
        in_specs=[pl.BlockSpec(memory_space=pl.ANY)] * 2,
        out_specs=pl.BlockSpec(memory_space=pltpu.VMEM),
        scratch_shapes=[
            pltpu.VMEM((rows, depth), left.dtype),
            pltpu.VMEM((2, steps, half, depth), left.dtype),
            pltpu.VMEM((b_rows * 2 * xs, columns), right.dtype),
            pltpu.VMEM((1, rows), jnp.float32),
            pltpu.VMEM((steps, 1, rows), jnp.float32),
            dma((2,)),
            dma((2, steps, PIECES)),
            dma((2, steps, PIECES)),
            dma((max(xs - 1, 1),)),
            dma((max(xs - 1, 1),)),
            dma((xs,)),
            dma((xs,)),
            dma((steps,)),
            dma((steps,)),
        ],
        compiler_params=pltpu.CompilerParams(
            collective_id=0, has_side_effects=True, vmem_limit_bytes=total + (8 << 20)
        ),
    )(left, right)


def solution(mesh):
    xs = mesh.shape["north"] // 2
    ys = xs
    order = ring_order(ys, mesh.shape["east"] // ys)
    placed = (P("north", "east"), P("north", "east"))
    return jax.shard_map(
        functools.partial(shards, xs, order),
        mesh=mesh, in_specs=placed, out_specs=P("north", "east"), check_vma=False,
    )
```

time: 147 us -> 54.9 us (0.37)
  waiting for transfers between devices: 104 us -> 0 us
  Pallas kernels: 0 us -> 51.3 us
  blocking collectives: 18.8 us -> 0 us
  between operations: 13.4 us -> 0.01 us
  matrix products: 6.55 us -> 0 us
  other arithmetic: 1.82 us -> 0 us
  local copies, waits for them, and re-layouts: 1.81 us -> 3.4 us
    all_gather x2 -> x0, waiting for transfers between devices: 103 us -> none  [the longest x1 76.8 us: shards(): left_line = lax.all_gather(left_factor, 'east', axis=1, tiled=True)]
    pallas_call x0 -> x1, Pallas kernels: none -> 51.3 us  [shards(): pl.pallas_call(functools.partial(kernel, xs, order), out_shape=jax.ShapeD...]
    psum x1 -> x0, blocking collectives: 18.8 us -> none  [shards(): row_power = lax.psum(jnp.sum(updated * updated, axis=1), 'east')]
    dot_general x1 -> x0, matrix products: 6.55 us -> none  [absorb_panel(): jnp.dot(left_panel, right_panel, preferred_element_type=jnp.float32)]
    unnamed x0 -> x5, local copies, waits for them, and re-layouts: none -> 3.4 us
    mul x1 -> x0, local copies, waits for them, and re-layouts: 1.81 us -> none  [shards(): updated * lax.rsqrt(row_power / (updated.shape[1] * lax.axis_size('east')...]
    mul x1 -> x0, other arithmetic: 1.81 us -> none  [shards(): updated * lax.rsqrt(row_power / (updated.shape[1] * lax.axis_size('east')...]
  transfers between devices with their start and end apart: 2 -> 0, of which waited for: 2 -> 0; matrix products, arithmetic and copies ran while one was open for 0% -> 0% of each run, Pallas kernels for 0% -> 0%
where the time goes in v1:
time: 54.9 us; the launch traced here: 54.7 us
  Pallas kernels  51.3 us (93%)
  local copies, waits for them, and re-layouts  3.4 us (6%)
    pallas_call x1, Pallas kernels, shards(): pl.pallas_call(functools.partial(kernel, xs, order), out_shape=jax.ShapeD...  51.3 us
    unnamed x5, local copies, waits for them, and re-layouts  3.4 us

profile of v1, /device:TPU:0, one launch (start us, length us, event | category | flops | bytes accessed | tf_op | source)
XLA Modules:
  0.0 54.7 jit_solution(7065360474091445764)
XLA Ops:
  0.0 0.0 copy-start
  0.0 1.0 %copy-done = bf16[1024,256]{1,0:T(8,128)(2,1)S(1)} copy-done((bf16[1024,256]{1,0:T(8,128)(2,1)S(1)}, bf16[1024,256]{1,0:T(8,128)(2,1)}, u32[]{:S(2)}) %copy-start) | copy-done | bytes 524312
  1.0 0.0 copy-start.1
  1.0 1.0 %copy-done.1 = bf16[512,512]{1,0:T(8,128)(2,1)S(1)} copy-done((bf16[512,512]{1,0:T(8,128)(2,1)S(1)}, bf16[512,512]{1,0:T(8,128)(2,1)}, u32[]{:S(2)}) %copy-start.1) | copy-done | bytes 524312
  2.1 51.3 %shard_map.28 = f32[1024,512]{1,0:T(8,128)S(1)} custom-call(bf16[1024,256]{1,0:T(8,128)(2,1)S(1)} %copy-done, bf16[512,512]{1,0:T(8,128)(2,1)S(1)} %copy-done.1), custom_call_target="tpu_custom_call" | custom-call | tf_op jit(solution)/shard_map/pallas_call | solution.py:211
  53.4 1.3 %copy.4 = f32[1024,512]{1,0:T(8,128)} copy(f32[1024,512]{1,0:T(8,128)S(1)} %shard_map.28) | data formatting | bytes 4194304
Async XLA Ops:
  0.0 1.0 %copy-start = (bf16[1024,256]{1,0:T(8,128)(2,1)S(1)}, bf16[1024,256]{1,0:T(8,128)(2,1)}, u32[]{:S(2)}) copy-start(bf16[1024,256]{1,0:T(8,128)(2,1)} %a_hbm.1) | copy-start | bytes 1572868
  1.0 1.0 %copy-start.1 = (bf16[512,512]{1,0:T(8,128)(2,1)S(1)}, bf16[512,512]{1,0:T(8,128)(2,1)}, u32[]{:S(2)}) copy-start(bf16[512,512]{1,0:T(8,128)(2,1)} %b_hbm.1) | copy-start | bytes 1572868

commit v2 on v1

--- a/solution.py
+++ b/solution.py
@@ -8,7 +8,7 @@
 from jax.sharding import PartitionSpec as P
 
 MESH = pl.DeviceIdType.MESH
-PIECES = 2
+PIECES = 4
 LANES = 128
 
 
@@ -108,96 +108,92 @@
         x_copies[0].start()
     c_copies[0].start()
 
-    def multiply(j, d, first, start, count):
+    waiting = [(j, d, c) for j in range(n - 1) for c in range(PIECES) for d in range(2)]
+
+    def rows_of(d, c):
+        return pl.ds(d * half + c * piece, piece)
+
+    def multiply(j, d, c):
         owner = at(-j if d == 0 else j)
-        b = right.at[pl.ds(pl.multiple_of(owner * depth, depth), depth)]
-
-        @pl.loop(0, count // piece)
-        def _(r):
-            begin = pl.multiple_of(start + r * piece, piece)
-            a_rows = pl.ds(begin, piece)
-            o_rows = pl.ds(pl.multiple_of(d * half + begin, piece), piece)
-            a = own[o_rows, :] if j == 0 else ring[d, j - 1, a_rows, :]
-            term = jnp.dot(a, b[...], preferred_element_type=jnp.float32)
-            if first:
-                out[o_rows, :] = term
-            else:
-                out[o_rows, :] += term
-
-    state = {"b": 1, "done": 0}
-
-    def b_stage():
-        t = state["b"]
+        b = right[pl.ds(pl.multiple_of(owner * depth, depth), depth), :]
+        a = own[rows_of(d, c), :] if j == 0 else ring[d, j - 1, pl.ds(c * piece, piece), :]
+        term = jnp.dot(a, b, preferred_element_type=jnp.float32)
+        return term if j == 0 else out[rows_of(d, c), :] + term
+
+    def b_stage(t):
         x_copies[t - 1].wait_recv()
         if t < xs - 1:
             x_copies[t].start()
         c_copies[t].start()
-        state["b"] += 1
-
-    def compute(limit, most):
+
+    def multiply_some(most, seen):
         for _ in range(most):
-            j = state["done"]
-            if j > limit:
+            if not waiting or (waiting[0][0] > 0 and (waiting[0][0] - 1, waiting[0][2], waiting[0][1]) > seen):
                 return
-            if j == 0:
+            j, d, c = waiting.pop(0)
+            if (j, d, c) == (0, 0, 0):
                 for t in range(xs):
                     c_copies[t].wait_recv()
-            for d in range(2):
-                multiply(j, d, j == 0, 0, half)
-            state["done"] += 1
-
+            out[rows_of(d, c), :] = multiply(j, d, c)
+
+    stage = 1
     for s in range(n - 2):
         for c in range(PIECES):
             for d in range(2):
                 a_copies[s, d, c].wait_recv()
                 a_copies[s + 1, d, c].start()
-        if s % 2 == 1 and state["b"] < xs:
-            b_stage()
-        elif state["b"] >= xs:
-            compute(s + 1, 2)
-    while state["b"] < xs:
-        b_stage()
-    compute(n - 2, n)
-
+                if stage < xs:
+                    if s >= 2 and s % 2 == 0 and (c, d) == (0, 1):
+                        b_stage(stage)
+                        stage += 1
+                elif c > 0 or s % 2:
+                    multiply_some(2, (s, c, d))
+    for t in range(stage, xs):
+        b_stage(t)
+    multiply_some(len(waiting), (n, 0, 0))
+
+    def s_copy(k, c):
+        return pltpu.make_async_remote_copy(
+            src_ref=sums_own.at[c], dst_ref=sums_in.at[k - 1, c],
+            send_sem=s_send.at[k - 1, c], recv_sem=s_recv.at[k - 1, c],
+            device_id=(me_north, lax.rem(me + k, n)), device_id_type=MESH,
+        )
+
+    s_copies = [[s_copy(k, c) for k in range(1, n)] for c in range(PIECES)]
     for c in range(PIECES):
         for d in range(2):
             a_copies[n - 2, d, c].wait_recv()
-            multiply(n - 1, d, False, c * piece, piece)
-            begin = d * half + c * piece
-            block = out[pl.ds(begin, piece), :]
-            block = block * block
-            narrow = block[:, :LANES]
+            if c > 0 and d == 0:
+                for copy in s_copies[c - 1]:
+                    copy.start()
+            total = multiply(n - 1, d, c)
+            out[rows_of(d, c), :] = total
+            total = total * total
+            narrow = total[:, :LANES]
             for k in range(LANES, columns, LANES):
-                narrow = narrow + block[:, k:k + LANES]
-            sums_own[:, pl.ds(begin, piece)] = jnp.sum(narrow.T, axis=0, keepdims=True)
+                narrow = narrow + total[:, k:k + LANES]
+            sums_own[c, :, d * piece:(d + 1) * piece] = jnp.sum(narrow.T, axis=0, keepdims=True)
 
     for copy in a_copies.values():
         copy.wait_send()
     for copy in x_copies + c_copies:
         copy.wait_send()
-
-    s_copies = [
-        pltpu.make_async_remote_copy(
-            src_ref=sums_own, dst_ref=sums_in.at[k - 1],
-            send_sem=s_send.at[k - 1], recv_sem=s_recv.at[k - 1],
-            device_id=(me_north, lax.rem(me + k, n)), device_id_type=MESH,
-        )
-        for k in range(1, n)
-    ]
-    for copy in s_copies:
+    for copy in s_copies[PIECES - 1]:
         copy.start()
-    for copy in s_copies:
-        copy.wait_recv()
-    power = sums_own[...]
-    for k in range(n - 1):
-        power = power + sums_in[k]
-    scale = lax.rsqrt(power / (columns * n) + 1e-06)
-    for begin in range(0, rows, piece):
-        gain = jnp.broadcast_to(scale[:, begin:begin + piece], (LANES, piece)).T
-        for k in range(0, columns, LANES):
-            out[pl.ds(begin, piece), k:k + LANES] *= gain
-    for copy in s_copies:
-        copy.wait_send()
+
+    for c in range(PIECES):
+        power = sums_own[c]
+        for k in range(1, n):
+            s_copies[c][k - 1].wait_recv()
+            power = power + sums_in[k - 1, c]
+        scale = lax.rsqrt(power / (columns * n) + 1e-06)
+        for d in range(2):
+            gain = jnp.broadcast_to(scale[:, d * piece:(d + 1) * piece], (LANES, piece)).T
+            for k in range(0, columns, LANES):
+                out[rows_of(d, c), k:k + LANES] *= gain
+    for line in s_copies:
+        for copy in line:
+            copy.wait_send()
 
 
 def shards(xs, order, left, right):
@@ -211,14 +207,14 @@
     return pl.pallas_call(
         functools.partial(kernel, xs, order),
         out_shape=jax.ShapeDtypeStruct((rows, columns), jnp.float32),
-        in_specs=[pl.BlockSpec(memory_space=pl.ANY)] * 2,
+        in_specs=[pl.BlockSpec(memory_space=pltpu.HBM)] * 2,
         out_specs=pl.BlockSpec(memory_space=pltpu.VMEM),
         scratch_shapes=[
             pltpu.VMEM((rows, depth), left.dtype),
             pltpu.VMEM((2, steps, half, depth), left.dtype),
             pltpu.VMEM((b_rows * 2 * xs, columns), right.dtype),
-            pltpu.VMEM((1, rows), jnp.float32),
-            pltpu.VMEM((steps, 1, rows), jnp.float32),
+            pltpu.VMEM((PIECES, 1, rows // PIECES), jnp.float32),
+            pltpu.VMEM((steps, PIECES, 1, rows // PIECES), jnp.float32),
             dma((2,)),
             dma((2, steps, PIECES)),
             dma((2, steps, PIECES)),
@@ -226,8 +222,8 @@
             dma((max(xs - 1, 1),)),
             dma((xs,)),
             dma((xs,)),
-            dma((steps,)),
-            dma((steps,)),
+            dma((steps, PIECES)),
+            dma((steps, PIECES)),
         ],
         compiler_params=pltpu.CompilerParams(
             collective_id=0, has_side_effects=True, vmem_limit_bytes=total + (8 << 20)

time: 54.9 us -> 55.7 us (1.015)
  Pallas kernels: 51.3 us -> 52 us
    pallas_call x1, Pallas kernels: 51.3 us -> 52 us  [shards(): pl.pallas_call(functools.partial(kernel, xs, order), out_shape=jax.ShapeD...]
where the time goes in v2:
time: 55.7 us; the launch traced here: 55.5 us
  Pallas kernels  52 us (93%)
  local copies, waits for them, and re-layouts  3.4 us (6%)
    pallas_call x1, Pallas kernels, shards(): pl.pallas_call(functools.partial(kernel, xs, order), out_shape=jax.ShapeD...  52 us
    unnamed x5, local copies, waits for them, and re-layouts  3.4 us

profile of v2, /device:TPU:0, one launch (start us, length us, event | category | flops | bytes accessed | tf_op | source)
XLA Modules:
  0.0 55.5 jit_solution(1357899565490591611)
XLA Ops:
  0.0 0.0 copy-start
  0.0 1.0 %copy-done = bf16[1024,256]{1,0:T(8,128)(2,1)S(1)} copy-done((bf16[1024,256]{1,0:T(8,128)(2,1)S(1)}, bf16[1024,256]{1,0:T(8,128)(2,1)}, u32[]{:S(2)}) %copy-start) | copy-done | bytes 524312
  1.0 0.0 copy-start.1
  1.0 1.0 %copy-done.1 = bf16[512,512]{1,0:T(8,128)(2,1)S(1)} copy-done((bf16[512,512]{1,0:T(8,128)(2,1)S(1)}, bf16[512,512]{1,0:T(8,128)(2,1)}, u32[]{:S(2)}) %copy-start.1) | copy-done | bytes 524312
  2.1 52.0 %shard_map.28 = f32[1024,512]{1,0:T(8,128)S(1)} custom-call(bf16[1024,256]{1,0:T(8,128)(2,1)S(1)} %copy-done, bf16[512,512]{1,0:T(8,128)(2,1)S(1)} %copy-done.1), custom_call_target="tpu_custom_call" | custom-call | tf_op jit(solution)/shard_map/pallas_call | solution.py:207
  54.1 1.3 %copy.4 = f32[1024,512]{1,0:T(8,128)} copy(f32[1024,512]{1,0:T(8,128)S(1)} %shard_map.28) | data formatting | bytes 4194304
Async XLA Ops:
  0.0 1.0 %copy-start = (bf16[1024,256]{1,0:T(8,128)(2,1)S(1)}, bf16[1024,256]{1,0:T(8,128)(2,1)}, u32[]{:S(2)}) copy-start(bf16[1024,256]{1,0:T(8,128)(2,1)} %a_hbm.1) | copy-start | bytes 1572868
  1.0 1.0 %copy-start.1 = (bf16[512,512]{1,0:T(8,128)(2,1)S(1)}, bf16[512,512]{1,0:T(8,128)(2,1)}, u32[]{:S(2)}) copy-start(bf16[512,512]{1,0:T(8,128)(2,1)} %b_hbm.1) | copy-start | bytes 1572868
